TPU v7x, 32 devices: a whole 2x2x4 slice. The times are simulated.
32 devices in a mesh: blk: 32 (over z, y, x, core).
Axes of the slice: x: 2, y: 2, z: 4, core: 2. Of those that a mesh axis runs over, the one named last changes fastest.
Arguments:
- defect: float32 [384, 128], P('blk'), may hold values from -6 to 6
- mass: float32 [384, 128], P('blk'), may hold values from 1 to 2
- block_diag: float32 [384, 128, 128], P('blk'), may hold values from -0.1875 to 0.1875
- coupling: float32 [3072, 128, 128], P('blk'), may hold values from -0.09375 to 0.09375
- tile_rows: int32 [3072], P('blk'), may hold values from 0 to 383, as said below
- tile_cols: int32 [3072], P('blk'), may hold values from 0 to 383, as said below
Outputs:
- update: float32 [384, 128], P('blk')
Inputs may be any that keep to these rules, and one draw needn't show every extreme that they name: `tile_rows`: block rows d * 12 to d * 12 + 11 belong to device d of blk, and each device holds the tiles at positions d * 96 to d * 96 + 95. Of every tile a device holds, exactly one of its block row and block column belongs to that device; the other belongs to a different device. Exactly half of the 96 tiles of every device have their block row with that device, and the other half their block column. A program may send only the blocks and products of tiles that exist; slots of a padded buffer that no tile fills need not be sent. `tile_cols`: of one device's tiles, at most 2 have their block column with any one other device and at most 2 have their block row with any one other device; every device reaches 2 with some other device on each of the two sides.
All inputs are finite; a program needn't handle non-finite values.
Results may differ from a plain program's by a relative error of at most 0.0001.
Values sent between devices are 32-bit elements; how exact they have to be, the bound alone decides.
A program may use at most 64 MiB of HBM per device.

v0:
```python
import functools

import jax
import jax.numpy as jnp
from jax import lax
from jax.experimental import pallas as pl
from jax.experimental.pallas import tpu as pltpu
from jax.sharding import PartitionSpec as P

ITERS = 3
F32 = jnp.float32
MESH = pl.DeviceIdType.MESH


def iota(shape, axis):
    return lax.broadcasted_iota(jnp.int32, shape, axis)


def iota_f(shape, axis):
    return iota(shape, axis).astype(F32)


def dot(hot, value):
    hot = hot.astype(jnp.bfloat16)
    out = None
    for _ in range(3):
        piece = value.astype(jnp.bfloat16)
        value = value - piece.astype(F32)
        term = lax.dot_general(
            hot, piece, (((1,), (0,)), ((), ())), preferred_element_type=F32
        )
        out = term if out is None else out + term
    return out


def total(value):
    return jnp.sum(jnp.sum(value, axis=0, keepdims=True), axis=1, keepdims=True)


def as_row(items):
    lane = iota((1, 128), 1)
    row = jnp.zeros((1, 128), F32)
    for index, item in enumerate(items):
        row = jnp.where(lane == index, item, row)
    return row


def pick(row, index):
    lane = iota((1, 128), 1)
    return jnp.sum(jnp.where(lane == index, row, 0.0), axis=1, keepdims=True)


def kernel(
    n,
    slots,
    defect_ref,
    mass_ref,
    diag_hbm,
    coup_hbm,
    rows_ref,
    cols_ref,
    out_ref,
    coup,
    diag,
    order_v,
    order_s,
    mass16,
    wbuf,
    xbuf,
    ask_hot,
    land_hot,
    send0,
    recv0,
    send_a,
    recv_a,
    send_b,
    recv_b,
    send_f,
    recv_f,
    load_sems,
    order_sem,
    sent,
    got,
):
    me = lax.axis_index("blk")
    rb, width = defect_ref.shape
    tiles = rows_ref.shape[1]
    half = tiles // 2
    pad = wbuf.shape[0]
    head = send0.shape[1]
    parts = 4
    chunk = tiles // parts

    loads = [pltpu.make_async_copy(diag_hbm, diag, load_sems.at[parts])]
    for part in range(parts):
        span = pl.ds(part * chunk, chunk)
        loads.append(
            pltpu.make_async_copy(coup_hbm.at[span], coup.at[span], load_sems.at[part])
        )
    for item in loads:
        item.start()

    barrier = pltpu.get_barrier_semaphore()

    def peer(k):
        there = me + k
        return jnp.where(there >= n, there - n, there)

    for k in range(1, n):
        pl.semaphore_signal(barrier, inc=1, device_id=(peer(k),), device_id_type=MESH)

    rows = rows_ref[...]
    cols = cols_ref[...]
    low = me * rb
    pushes = (rows < low) | (rows >= low + rb)
    push_l = jnp.where(pushes, 1.0, 0.0)
    rem_l = jnp.where(pushes, rows, cols).astype(F32)
    loc_l = (jnp.where(pushes, cols, rows) - low).astype(F32)
    own_l = jnp.floor((rem_l + 0.5) * (1.0 / rb))
    far_l = rem_l - own_l * rb
    me_f = me.astype(F32)
    rel_l = own_l - me_f - 1.0
    rel_l = jnp.where(rel_l < 0.0, rel_l + n, rel_l)
    key_l = own_l + push_l * n
    square = (tiles, tiles)
    eye = iota(square, 0) == iota(square, 1)

    def to_s(value):
        return jnp.sum(jnp.where(eye, value, 0.0), axis=1, keepdims=True)

    earlier = iota(square, 0) < iota(square, 1)
    key_s = to_s(key_l)
    push_s = to_s(push_l)
    slot_l = jnp.sum(
        jnp.where((key_s == key_l) & earlier, 1.0, 0.0), axis=0, keepdims=True
    )
    pos_l = jnp.sum(
        jnp.where((push_s < push_l) | ((push_s == push_l) & earlier), 1.0, 0.0),
        axis=0,
        keepdims=True,
    )
    pos_s = to_s(pos_l)
    slot_s = to_s(slot_l)
    own_s = to_s(own_l)
    far_s = to_s(far_l)
    loc_s = to_s(loc_l)
    lines = slots + 1
    u_l = rel_l * lines + slot_l
    u_s = to_s(rel_l * slots + slot_l)
    wide = (tiles, 128)
    lane_w = iota_f(wide, 1)
    push_int = jnp.where(pushes, 1, 0)
    push_down = jnp.sum(jnp.where(eye, push_int, 0), axis=1, keepdims=True)
    place = jnp.sum(
        jnp.where(
            (push_down < push_int) | ((push_down == push_int) & earlier), 1, 0
        ),
        axis=0,
        keepdims=True,
    )
    place_down = jnp.sum(jnp.where(eye, place, 0), axis=1, keepdims=True)
    order_v[...] = jnp.sum(
        jnp.where(place_down == iota(wide, 1), iota(wide, 0), 0), axis=0, keepdims=True
    )
    order_copy = pltpu.make_async_copy(order_v, order_s, order_sem)
    order_copy.start()
    lane_1 = iota_f((1, 128), 1)
    push_u = jnp.sum(jnp.where(pos_s == lane_w + half, u_s, 0.0), axis=0, keepdims=True)
    push_u = jnp.where(lane_1 < half, push_u, -1.0)
    fetch_row = jnp.sum(jnp.where(pos_s == lane_w, loc_s, 0.0), axis=0, keepdims=True)
    fetch_row = jnp.where(lane_1 < half, fetch_row, -1.0)
    sorted_shape = (half, tiles)
    fetch_here = pos_l == iota_f(sorted_shape, 0)
    push_here = pos_l == iota_f(sorted_shape, 0) + half
    fetch_u = jnp.sum(jnp.where(fetch_here, u_l, 0.0), axis=1, keepdims=True)
    fetch_v = jnp.sum(
        jnp.where(fetch_here, rel_l * head + far_l, 0.0), axis=1, keepdims=True
    )
    push_col = jnp.sum(jnp.where(push_here, loc_l, 0.0), axis=1, keepdims=True)
    lane_key = own_s * slots + slot_s
    asks = jnp.sum(
        jnp.where((lane_key == lane_w) & (push_s < 0.5), far_s + 1.0, 0.0),
        axis=0,
        keepdims=True,
    ) - 1.0
    goals = jnp.sum(
        jnp.where((lane_key == lane_w) & (push_s > 0.5), far_s + 1.0, 0.0),
        axis=0,
        keepdims=True,
    ) - 1.0
    lines_all = n * lines
    slots_all = n * slots

    def hot(mask):
        return jnp.where(mask, 1.0, 0.0)

    wbuf[...] = jnp.zeros(wbuf.shape, F32)
    wbuf[0:rb, :] = -defect_ref[...]
    mass16[...] = jnp.zeros(mass16.shape, F32)
    mass16[0:rb, :] = mass_ref[...]
    vector = wbuf[...]
    send0[...] = jnp.zeros(send0.shape, F32)
    send0[0, 0:rb, :] = -defect_ref[...]
    own_part = as_row([total(vector * vector)])
    send0[0, rb : rb + 1, :] = own_part
    send0[0, rb + 1 : rb + 2, :] = asks
    send0[0, rb + 2 : rb + 3, :] = goals
    recv0[n - 1] = jnp.zeros(recv0.shape[1:], F32)
    for turn in range(ITERS):
        recv_b[turn, slots_all - slots : slots_all] = jnp.zeros((slots, 1, 128), F32)
    for turn in range(ITERS - 1):
        recv_a[turn, lines_all - lines : lines_all] = jnp.zeros((lines, 1, 128), F32)
    recv_f[n - 1] = jnp.zeros((1, 128), F32)

    pl.semaphore_wait(barrier, n - 1)

    def broadcast(source, target, index, count, spread):
        for k in range(1, n):
            start = (n - 1 - k) * count
            pltpu.make_async_remote_copy(
                src_ref=source.at[pl.ds((k - 1) * count, count)] if spread else source,
                dst_ref=target.at[pl.ds(start, count)],
                send_sem=sent.at[index],
                recv_sem=got.at[index],
                device_id=(peer(k),),
                device_id_type=MESH,
            ).start()

    def await_all(target, sem, count):
        view = target.at[pl.ds(0, (n - 1) * count)]
        pltpu.make_async_copy(view, view, sem).wait()

    broadcast(send0, recv0, 0, 1, False)

    spread_hot = hot(iota_f((slots_all, 128), 0) == push_u)
    fetch_hot = hot(iota_f((half, lines_all), 1) == fetch_u)
    first_hot = hot(iota_f((half, n * head), 1) == fetch_v)
    input_hot = hot(iota_f((half, pad), 1) == push_col)
    kept_hot = hot(iota_f((pad, 128), 0) == fetch_row)

    lane_k = iota((width, 128), 1)

    def matvec(acc, tile, index):
        row = xbuf[index : index + 1, :]
        value = jnp.sum(tile * row, axis=1, keepdims=True)
        return jnp.where(lane_k == index, value, acc)

    def coupled(base, acc):
        for index in range(half):
            tile = jnp.clip(order_s[0, base + index], 0, 2 * half - 1)
            acc = matvec(acc, coup[tile], index)
        return acc

    empty = jnp.zeros((width, 128), F32)

    def begin(turn, vector):
        xbuf[0:half, :] = dot(input_hot, vector)
        found = coupled(half, empty).T
        send_b[turn, :, 0, :] = dot(spread_hot, found)
        broadcast(send_b.at[turn], recv_b.at[turn], 1 + 2 * turn, slots, True)
        wbuf[...] = vector
        acc = empty
        for index in range(rb):
            value = jnp.sum(diag[index] * wbuf[index : index + 1, :], axis=1, keepdims=True)
            acc = jnp.where(lane_k == half + index, value, acc)
        return mass16[...] * vector, acc

    def finish(turn, started, inputs):
        image, acc = started
        xbuf[0:half, :] = inputs
        found = coupled(0, acc).T
        image = image + dot(kept_hot, found) + found[half : half + pad, :]
        await_all(recv_b.at[turn], got.at[1 + 2 * turn], slots)
        return image + dot(land_hot[...], recv_b[turn, :, 0, :])

    for item in loads:
        item.wait()
    order_copy.wait()

    started = begin(0, vector)
    await_all(recv0, got.at[0], 1)

    def addressed(offset, count):
        size = n * count
        line = recv0[:, rb + offset : rb + offset + 1, :].reshape(n, 128)
        owner = jnp.floor((iota_f((size, n), 0) + 0.5) * (1.0 / count))
        spread = dot(hot(owner == iota_f((size, n), 1)), line + 1.0)
        row = iota_f((size, 128), 0)
        owner = jnp.floor((row + 0.5) * (1.0 / count))
        slot = row - owner * count
        lane = iota_f((size, 128), 1)
        mine = (lane == me_f * slots + slot) & (slot < slots) & (owner < n - 1)
        found = jnp.sum(jnp.where(mine, spread, 0.0), axis=1, keepdims=True) - 1.0
        return hot(found == lane)

    land_hot[...] = addressed(2, slots).T[0:pad, :]
    ask_hot[...] = addressed(1, lines)
    squares = jnp.sum(recv0[:, rb, :], axis=0, keepdims=True) + own_part
    beta = jnp.sqrt(pick(squares, 0))
    inputs = dot(first_hot, recv0[...].reshape(n * head, 128))
    image = finish(0, started, inputs)
    basis = [vector / beta]
    images = [image / beta]
    heads = []
    gram = {}

    for turn in range(1, ITERS):
        vector = images[-1]
        own_part = as_row(
            [total(vector * item) for item in basis]
            + [total(vector * item) for item in images]
        )
        wide_vector = jnp.concatenate([vector, jnp.zeros((128 - pad, 128), F32)], axis=0)
        blocks = dot(ask_hot[...], wide_vector)
        row = iota_f((lines_all, 128), 0)
        slot = row - jnp.floor((row + 0.5) * (1.0 / lines)) * lines
        send_a[turn - 1, :, 0, :] = jnp.where(slot == slots, own_part, blocks)
        broadcast(send_a.at[turn - 1], recv_a.at[turn - 1], 2 * turn, lines, True)
        started = begin(turn, vector)
        await_all(recv_a.at[turn - 1], got.at[2 * turn], lines)
        came = recv_a[turn - 1, :, 0, :]
        sums = jnp.sum(jnp.where(slot == slots, came, 0.0), axis=0, keepdims=True)
        sums = sums + own_part
        image = finish(turn, started, dot(fetch_hot, came))
        dots = [pick(sums, index) for index in range(turn)]
        for index in range(turn):
            gram[index, turn - 1] = pick(sums, turn + index)
        heads.append(dots[0])
        square = gram[turn - 1, turn - 1]
        left = square
        for value in dots:
            left = left - value * value
        scale = lax.rsqrt(jnp.maximum(left, square * 1e-6))
        for index in range(turn):
            vector = vector - dots[index] * basis[index]
            image = image - dots[index] * images[index]
        basis.append(vector * scale)
        images.append(image * scale)

    vector = images[-1]
    own_part = as_row(
        [total(vector * basis[0])] + [total(vector * item) for item in images]
    )
    send_f[0] = own_part
    broadcast(send_f, recv_f, 2 * ITERS, 1, False)
    await_all(recv_f, got.at[2 * ITERS], 1)
    sums = jnp.sum(recv_f[:, 0, :], axis=0, keepdims=True) + own_part
    heads.append(pick(sums, 0))
    for index in range(ITERS):
        gram[index, ITERS - 1] = pick(sums, 1 + index)

    factor = {}
    for i in range(ITERS):
        for j in range(i + 1):
            value = gram[j, i]
            for k in range(j):
                value = value - factor[i, k] * factor[j, k]
            factor[i, j] = jnp.sqrt(value) if i == j else value / factor[j, j]
    forward = []
    for i in range(ITERS):
        value = beta * heads[i]
        for k in range(i):
            value = value - factor[i, k] * forward[k]
        forward.append(value / factor[i, i])
    mixing = [None] * ITERS
    for i in reversed(range(ITERS)):
        value = forward[i]
        for k in range(i + 1, ITERS):
            value = value - factor[k, i] * mixing[k]
        mixing[i] = value / factor[i, i]
    update = mixing[0] * basis[0]
    for i in range(1, ITERS):
        update = update + mixing[i] * basis[i]
    out_ref[...] = update[0:rb, :]

    await_all(recv0, sent.at[0], 1)
    for turn in range(ITERS):
        await_all(send_b.at[turn], sent.at[1 + 2 * turn], slots)
    for turn in range(1, ITERS):
        await_all(send_a.at[turn - 1], sent.at[2 * turn], lines)
    await_all(recv_f, sent.at[2 * ITERS], 1)


def on_device(defect, mass, block_diag, coupling, tile_rows, tile_cols):
    rb, width = defect.shape
    tiles = tile_rows.shape[0]
    n = lax.axis_size("blk")
    slots = (tiles // 2 + n - 2) // (n - 1)
    pad = -(-rb // 8) * 8
    head = -(-(rb + 3) // 8) * 8
    vmem = pl.BlockSpec(memory_space=pltpu.VMEM)
    hbm = pl.BlockSpec(memory_space=pl.ANY)
    return pl.pallas_call(
        functools.partial(kernel, n, slots),
        out_shape=jax.ShapeDtypeStruct((rb, width), F32),
        in_specs=[vmem, vmem, hbm, hbm, vmem, vmem],
        out_specs=vmem,
        scratch_shapes=[
            pltpu.VMEM((tiles, width, width), F32),
            pltpu.VMEM((rb, width, width), F32),
            pltpu.VMEM((1, 128), jnp.int32),
            pltpu.SMEM((1, 128), jnp.int32),
            pltpu.VMEM((pad, width), F32),
            pltpu.VMEM((pad, width), F32),
            pltpu.VMEM((tiles, width), F32),
            pltpu.VMEM((n * (slots + 1), 128), F32),
            pltpu.VMEM((pad, n * slots), F32),
            pltpu.VMEM((1, head, width), F32),
            pltpu.VMEM((n, head, width), F32),
            pltpu.VMEM((ITERS - 1, n * (slots + 1), 1, width), F32),
            pltpu.VMEM((ITERS - 1, n * (slots + 1), 1, width), F32),
            pltpu.VMEM((ITERS, n * slots, 1, width), F32),
            pltpu.VMEM((ITERS, n * slots, 1, width), F32),
            pltpu.VMEM((1, 1, width), F32),
            pltpu.VMEM((n, 1, width), F32),
            pltpu.SemaphoreType.DMA((5,)),
            pltpu.SemaphoreType.DMA,
            pltpu.SemaphoreType.DMA((2 * ITERS + 1,)),
            pltpu.SemaphoreType.DMA((2 * ITERS + 1,)),
        ],
        compiler_params=pltpu.CompilerParams(collective_id=0, has_side_effects=True),
    )(
        defect,
        mass,
        block_diag,
        coupling,
        tile_rows.reshape(1, tiles),
        tile_cols.reshape(1, tiles),
    )


def solution(mesh):
    in_specs = (
        P("blk", None),
        P("blk", None),
        P("blk", None, None),
        P("blk", None, None),
        P("blk"),
        P("blk"),
    )
    return jax.shard_map(
        on_device, mesh=mesh, in_specs=in_specs, out_specs=P("blk", None), check_vma=False
    )
```

profile of v0, /device:TPU:0, one launch (start us, length us, event | category | flops | bytes accessed | tf_op | source)
XLA Modules:
  0.0 37.7 jit_solution(16521565179822553676)
XLA Ops:
  0.0 36.4 %shard_map.64 = f32[12,128]{1,0:T(8,128)} custom-call(f32[12,128]{1,0:T(8,128)} %defect_ref.1, f32[12,128]{1,0:T(8,128)} %mass_ref.1, f32[12,128,128]{2,1,0:T(8,128)} %diag_hbm.1, f32[96,128,128]{2,1,0:T(8,128)} %coup_hbm.1, s32[1,96]{1,0:T(1,128)} %bitcast.2, s32[1,96]{1,0:T(1,128)} %bitcast.3), custom_call_target="tpu_custom_call" | custom-call | tf_op jit(solution)/shard_map/pallas_call | solution.py:393
  36.4 1.3 %copy.8 = f32[12,128]{1,0:T(8,128)} copy(f32[12,128]{1,0:T(8,128)} %shard_map.64) | data formatting | bytes 12288
where the time goes:
time: 37.9 us; the launch traced here: 37.7 us
  Pallas kernels  36.4 us (96%)
  local copies, waits for them, and re-layouts  1.3 us (3%)
    pallas_call x1, Pallas kernels, on_device(): pl.pallas_call(functools.partial(kernel, n, slots), out_shape=jax.ShapeDt...  36.4 us
    unnamed x1, local copies, waits for them, and re-layouts  1.3 us

commit v1 on v0

v1 whole, which is shorter than its diff:
```python
import functools

import jax
import jax.numpy as jnp
from jax import lax
from jax.experimental import pallas as pl
from jax.experimental.pallas import tpu as pltpu
from jax.sharding import PartitionSpec as P

ITERS = 3
F32 = jnp.float32
I32 = jnp.int32
MESH = pl.DeviceIdType.MESH
BASE = 64
VMEM_LIMIT = 48 * 1024 * 1024


def iota(shape, axis):
    return lax.broadcasted_iota(I32, shape, axis)


def iota_f(shape, axis):
    return iota(shape, axis).astype(F32)


def total(value):
    return jnp.sum(jnp.sum(value, axis=0, keepdims=True), axis=1, keepdims=True)


def as_row(items):
    lane = iota((1, 128), 1)
    row = jnp.zeros((1, 128), F32)
    for index, item in enumerate(items):
        row = jnp.where(lane == index, item, row)
    return row


def pick(row, index):
    lane = iota((1, 128), 1)
    return jnp.sum(jnp.where(lane == index, row, 0.0), axis=1, keepdims=True)


def ranges(n):
    cuts = [0, 2, 6, 10, n // 2, n - n // 4, n - 1]
    cuts = sorted({min(cut, n - 1) for cut in cuts})
    return list(zip(cuts[:-1], cuts[1:]))


def kernel(
    n,
    slots,
    defect_hbm,
    mass_hbm,
    diag_hbm,
    coup_hbm,
    rows_hbm,
    cols_hbm,
    out_ref,
    coup,
    diag,
    defect_ref,
    mass_ref,
    rows_ref,
    cols_ref,
    table_v,
    table,
    wbuf,
    codes,
    ask_ref,
    goal_ref,
    send0,
    recv0,
    blocks,
    send_a,
    recv_a,
    send_b,
    recv_b,
    send_f,
    recv_f,
    load_sems,
    table_sem,
    sent,
    got,
):
    me = lax.axis_index("blk")
    rb, width = defect_ref.shape
    tiles = rows_ref.shape[1]
    pad = wbuf.shape[0]
    lanes = table.shape[1]
    parts = 4
    chunk = tiles // parts
    groups = ranges(n)
    count = len(groups)
    head = rb + 1
    lines = slots + 1

    peers = {0: me}
    for mask in range(1, n):
        low_bit = mask & -mask
        sign = 1 - 2 * ((me // low_bit) % 2)
        peers[mask] = peers[mask - low_bit] + sign * low_bit
    peer = [peers[n - 1 - place] for place in range(n)]

    small = [
        pltpu.make_async_copy(rows_hbm, rows_ref, load_sems.at[parts + 1]),
        pltpu.make_async_copy(cols_hbm, cols_ref, load_sems.at[parts + 2]),
        pltpu.make_async_copy(defect_hbm, defect_ref, load_sems.at[parts + 3]),
        pltpu.make_async_copy(mass_hbm, mass_ref, load_sems.at[parts + 4]),
    ]
    for item in small:
        item.start()

    barrier = pltpu.get_barrier_semaphore()
    for place in range(n - 1):
        pl.semaphore_signal(barrier, inc=1, device_id=(peer[place],), device_id_type=MESH)

    loads = []
    for part in range(parts):
        span = pl.ds(part * chunk, chunk)
        loads.append(
            pltpu.make_async_copy(coup_hbm.at[span], coup.at[span], load_sems.at[part])
        )
    loads.append(pltpu.make_async_copy(diag_hbm, diag, load_sems.at[parts]))
    for item in loads:
        item.start()
    for item in small:
        item.wait()

    rows = rows_ref[...]
    cols = cols_ref[...]
    low = me * rb
    pushes = (rows < low) | (rows >= low + rb)
    push_l = jnp.where(pushes, 1, 0)
    rem_l = jnp.where(pushes, rows, cols)
    loc_l = jnp.where(pushes, cols, rows) - low
    own_l = (rem_l * (-(-65536 // rb))) >> 16
    far_l = rem_l - own_l * rb
    square = (tiles, tiles)
    eye = iota(square, 0) == iota(square, 1)
    earlier = iota(square, 0) < iota(square, 1)

    def to_s(value, zero):
        return jnp.sum(jnp.where(eye, value, zero), axis=1, keepdims=True)

    key_l = own_l + push_l * n
    key_s = to_s(key_l, 0)
    slot_l = jnp.sum(jnp.where((key_s == key_l) & earlier, 1, 0), axis=0, keepdims=True)
    line_l = (n - 1 - (own_l ^ me)) * slots + slot_l
    tile_l = iota((1, tiles), 1)
    line_s = to_s(line_l + push_l * lanes, 0)
    pack_s = to_s(((tile_l * BASE + loc_l) * BASE + far_l) + 1, 0)
    name_s = to_s(own_l * slots + slot_l, 0)
    code_s = to_s(jnp.where(pushes, (far_l + 1) * BASE, far_l + 1).astype(F32), 0.0)
    wide = (tiles, lanes)
    lane_w = iota(wide, 1)
    kinds = []
    for kind in range(2):
        here = line_s == lane_w + kind * lanes
        packed = jnp.sum(jnp.where(here, pack_s, 0), axis=0, keepdims=True)
        there = packed > 0
        packed = jnp.where(there, packed - 1, 0)
        local = jnp.clip((packed >> 6) & (BASE - 1), 0, rb - 1)
        kinds.append(jnp.clip(packed >> 12, 0, tiles - 1))
        kinds.append(jnp.where(there, local, BASE) if kind == 0 else local)
        if kind == 0:
            kinds.append(jnp.clip(packed & (BASE - 1), 0, rb - 1))
    for index, value in enumerate(kinds):
        table_v[index : index + 1, :] = value
    table_copy = pltpu.make_async_copy(table_v, table, table_sem)
    table_copy.start()
    code = jnp.sum(jnp.where(name_s == lane_w, code_s, 0.0), axis=0, keepdims=True)
    code = code[:, 0:128]

    wbuf[...] = jnp.zeros(wbuf.shape, F32)
    wbuf[0:rb, :] = -defect_ref[...]
    vector = wbuf[...]
    lane_1 = iota((1, 128), 1)
    code = jnp.where(lane_1 == me * slots, total(vector * vector), code)
    send0[0:rb, 0, :] = -defect_ref[...]
    send0[rb, :, :] = code
    codes[n - 1 : n, :] = code

    pl.semaphore_wait(barrier, n - 1)

    def send(phase, group, source, target, size, spread):
        for place in range(*groups[group]):
            span = pl.ds(place * size, size)
            pltpu.make_async_remote_copy(
                src_ref=source.at[span] if spread else source,
                dst_ref=target.at[span],
                send_sem=sent.at[phase],
                recv_sem=got.at[phase, group],
                device_id=(peer[place],),
                device_id_type=MESH,
            ).start()

    def await_group(phase, group, target, size):
        first, last = groups[group]
        view = target.at[pl.ds(first * size, (last - first) * size)]
        pltpu.make_async_copy(view, view, got.at[phase, group]).wait()

    def await_sent(phase, target, size):
        view = target.at[pl.ds(0, (n - 1) * size)]
        pltpu.make_async_copy(view, view, sent.at[phase]).wait()

    for group in range(count):
        send(0, group, send0, recv0, head, False)

    lane_k = iota((width, 128), 1)
    sub = iota((pad, 128), 0)
    sub_f = sub.astype(F32)
    empty = jnp.zeros((width, 128), F32)

    def slots_of(group):
        first, last = groups[group]
        return [(place, slot) for place in range(first, last) for slot in range(slots)]

    def product(tile, row):
        return jnp.sum(tile * row, axis=1, keepdims=True)

    def push_sums(group):
        acc = empty
        for index, (place, slot) in enumerate(slots_of(group)):
            line = place * slots + slot
            row = wbuf[pl.ds(table[4, line], 1), :]
            acc = jnp.where(lane_k == index, product(coup[table[3, line]], row), acc)
        return acc

    def push_out(turn, group, acc):
        found = acc.T
        for index, (place, slot) in enumerate(slots_of(group)):
            send_b[turn, place * slots + slot, :, :] = found[index : index + 1, :]
        send(1 + 2 * turn, group, send_b.at[turn], recv_b.at[turn], slots, True)

    def push_all(turn):
        held = push_sums(0)
        for group in range(count):
            later = push_sums(group + 1) if group + 1 < count else None
            push_out(turn, group, held)
            held = later

    def fetch_sums(group, source):
        acc = empty
        for index, (place, slot) in enumerate(slots_of(group)):
            line = place * slots + slot
            row = source(place, slot)
            acc = jnp.where(lane_k == index, product(coup[table[0, line]], row), acc)
        return acc

    def fetch_in(group, image, acc):
        found = acc.T
        for index, (place, slot) in enumerate(slots_of(group)):
            here = sub == table[1, place * slots + slot]
            image = image + jnp.where(here, found[index : index + 1, :], 0.0)
        return image

    def fetch_all(image, ready, source):
        held = None
        for group in near_first:
            ready(group)
            sums = fetch_sums(group, source)
            if held is not None:
                image = fetch_in(group + 1, image, held)
            held = sums
        return fetch_in(0, image, held)

    def own_rows(image):
        acc = empty
        for index in range(rb):
            value = product(diag[index], wbuf[index : index + 1, :])
            acc = jnp.where(lane_k == index, value, acc)
        return image + acc.T[0:pad, :]

    def land_group(turn, group, image):
        for place, slot in slots_of(group):
            here = goal_ref[slot, place : place + 1, :] == sub_f
            line = recv_b[turn, place * slots + slot, :, :]
            image = image + jnp.where(here, line, 0.0)
        return image

    def decode(first, last):
        shape = (last - first, 128)
        found = codes[first:last, :]
        lane = iota(shape, 1)
        for slot in range(slots):
            mine = jnp.where(lane == me * slots + slot, found, 0.0)
            value = jnp.sum(mine, axis=1, keepdims=True)
            goal = jnp.floor(value * (1.0 / BASE))
            goal_ref[slot, first:last, :] = jnp.broadcast_to(goal - 1.0, shape)
            ask_ref[slot, first:last, :] = jnp.broadcast_to(value - goal * BASE - 1.0, shape)

    def gather_group(turn, group, vector):
        for place, slot in slots_of(group):
            here = ask_ref[slot, place : place + 1, :] == sub_f
            line = jnp.sum(jnp.where(here, vector, 0.0), axis=0, keepdims=True)
            send_a[turn - 1, place * lines + slot, :, :] = line

    def send_asked(turn, group, own_part):
        for place in range(*groups[group]):
            send_a[turn - 1, place * lines + slots, :, :] = own_part
        send(2 * turn, group, send_a.at[turn - 1], recv_a.at[turn - 1], lines, True)

    for item in loads:
        item.wait()
    table_copy.wait()
    mass = jnp.concatenate([mass_ref[...], jnp.zeros((pad - rb, 128), F32)], axis=0)

    near_first = list(reversed(range(count)))
    push_all(0)
    image = own_rows(mass * vector)

    def ready_first(group):
        await_group(0, group, recv0, head)
        for place in range(*groups[group]):
            codes[place : place + 1, :] = recv0[place * head + rb]
            for row in range(rb):
                blocks[place * rb + row, :, :] = recv0[place * head + row]

    def block_row(place, slot):
        return blocks[place * rb + table[2, place * slots + slot]]

    image = fetch_all(image, ready_first, block_row)
    decode(0, n)
    whose = (n - 1 - iota((n, 128), 0)) ^ me
    squares = total(jnp.where(iota((n, 128), 1) == whose * slots, codes[...], 0.0))
    beta = jnp.sqrt(squares)
    for group in near_first:
        await_group(1, group, recv_b.at[0], slots)
        image = land_group(0, group, image)
    basis = [vector / beta]
    images = [image / beta]
    heads = []
    gram = {}

    for turn in range(1, ITERS):
        vector = images[-1]
        wbuf[...] = vector
        own_part = as_row(
            [total(vector * item) for item in basis]
            + [total(vector * item) for item in images]
        )
        for group in range(count):
            gather_group(turn, group, vector)
            send_asked(turn, group, own_part)
        push_all(turn)
        image = own_rows(mass * vector)
        parts_of = [own_part]

        def ready(group):
            await_group(2 * turn, group, recv_a.at[turn - 1], lines)
            for place in range(*groups[group]):
                parts_of.append(recv_a[turn - 1, place * lines + slots, :, :])

        def asked_row(place, slot):
            return recv_a[turn - 1, place * lines + slot, :, :]

        image = fetch_all(image, ready, asked_row)
        sums = sum(parts_of[1:], parts_of[0])
        dots = [pick(sums, index) for index in range(turn)]
        for index in range(turn):
            gram[index, turn - 1] = pick(sums, turn + index)
        heads.append(dots[0])
        square = gram[turn - 1, turn - 1]
        left = square
        for value in dots:
            left = left - value * value
        scale = lax.rsqrt(jnp.maximum(left, square * 1e-6))
        for index in range(turn):
            vector = vector - dots[index] * basis[index]
        basis.append(vector * scale)
        for group in near_first:
            await_group(1 + 2 * turn, group, recv_b.at[turn], slots)
            image = land_group(turn, group, image)
        for index in range(turn):
            image = image - dots[index] * images[index]
        images.append(image * scale)

    vector = images[-1]
    own_part = as_row(
        [total(vector * basis[0])] + [total(vector * item) for item in images]
    )
    send_f[0] = own_part
    last_phase = 2 * ITERS
    for group in range(count):
        send(last_phase, group, send_f, recv_f, 1, False)
    sums = own_part
    for group in near_first:
        await_group(last_phase, group, recv_f, 1)
        for place in range(*groups[group]):
            sums = sums + recv_f[place, :, :]
    heads.append(pick(sums, 0))
    for index in range(ITERS):
        gram[index, ITERS - 1] = pick(sums, 1 + index)

    factor = {}
    for i in range(ITERS):
        for j in range(i + 1):
            value = gram[j, i]
            for k in range(j):
                value = value - factor[i, k] * factor[j, k]
            factor[i, j] = jnp.sqrt(value) if i == j else value / factor[j, j]
    forward = []
    for i in range(ITERS):
        value = beta * heads[i]
        for k in range(i):
            value = value - factor[i, k] * forward[k]
        forward.append(value / factor[i, i])
    mixing = [None] * ITERS
    for i in reversed(range(ITERS)):
        value = forward[i]
        for k in range(i + 1, ITERS):
            value = value - factor[k, i] * mixing[k]
        mixing[i] = value / factor[i, i]
    update = mixing[0] * basis[0]
    for i in range(1, ITERS):
        update = update + mixing[i] * basis[i]
    out_ref[...] = update[0:rb, :]

    await_sent(0, recv0, head)
    for turn in range(ITERS):
        await_sent(1 + 2 * turn, recv_b.at[turn], slots)
    for turn in range(1, ITERS):
        await_sent(2 * turn, recv_a.at[turn - 1], lines)
    await_sent(last_phase, recv_f, 1)


def on_device(defect, mass, block_diag, coupling, tile_rows, tile_cols):
    rb, width = defect.shape
    tiles = tile_rows.shape[0]
    n = lax.axis_size("blk")
    slots = (tiles // 2 + n - 2) // (n - 1)
    lines = slots + 1
    pad = -(-rb // 8) * 8
    lanes = -(-n * slots // 128) * 128
    hbm = pl.BlockSpec(memory_space=pltpu.HBM)
    phases = 2 * ITERS + 1
    return pl.pallas_call(
        functools.partial(kernel, n, slots),
        out_shape=jax.ShapeDtypeStruct((rb, width), F32),
        in_specs=[hbm] * 6,
        out_specs=pl.BlockSpec(memory_space=pltpu.VMEM),
        scratch_shapes=[
            pltpu.VMEM((tiles, width, width), F32),
            pltpu.VMEM((rb, width, width), F32),
            pltpu.VMEM((rb, width), F32),
            pltpu.VMEM((rb, width), F32),
            pltpu.VMEM((1, tiles), I32),
            pltpu.VMEM((1, tiles), I32),
            pltpu.VMEM((8, lanes), I32),
            pltpu.SMEM((8, lanes), I32),
            pltpu.VMEM((pad, width), F32),
            pltpu.VMEM((n, width), F32),
            pltpu.VMEM((slots, n, width), F32),
            pltpu.VMEM((slots, n, width), F32),
            pltpu.VMEM((rb + 1, 1, width), F32),
            pltpu.VMEM((n * (rb + 1), 1, width), F32),
            pltpu.VMEM((n * rb, 1, width), F32),
            pltpu.VMEM((ITERS - 1, n * lines, 1, width), F32),
            pltpu.VMEM((ITERS - 1, n * lines, 1, width), F32),
            pltpu.VMEM((ITERS, n * slots, 1, width), F32),
            pltpu.VMEM((ITERS, n * slots, 1, width), F32),
            pltpu.VMEM((1, 1, width), F32),
            pltpu.VMEM((n, 1, width), F32),
            pltpu.SemaphoreType.DMA((9,)),
            pltpu.SemaphoreType.DMA,
            pltpu.SemaphoreType.DMA((phases,)),
            pltpu.SemaphoreType.DMA((phases, len(ranges(n)))),
        ],
        compiler_params=pltpu.CompilerParams(
            collective_id=0, has_side_effects=True, vmem_limit_bytes=VMEM_LIMIT
        ),
    )(
        defect,
        mass,
        block_diag,
        coupling,
        tile_rows.reshape(1, tiles),
        tile_cols.reshape(1, tiles),
    )


def solution(mesh):
    in_specs = (
        P("blk", None),
        P("blk", None),
        P("blk", None, None),
        P("blk", None, None),
        P("blk"),
        P("blk"),
    )
    return jax.shard_map(
        on_device, mesh=mesh, in_specs=in_specs, out_specs=P("blk", None), check_vma=False
    )
```

time: 37.9 us -> 35.8 us (0.945)
  Pallas kernels: 36.4 us -> 31 us
  local copies, waits for them, and re-layouts: 1.3 us -> 4.44 us
    pallas_call x1, Pallas kernels: 36.4 us -> 31 us  [on_device(): pl.pallas_call(functools.partial(kernel, n, slots), out_shape=jax.ShapeDt...]
    unnamed x1 -> x11, local copies, waits for them, and re-layouts: 1.3 us -> 4.44 us
where the time goes in v1:
time: 35.8 us; the launch traced here: 35.5 us
  Pallas kernels  31 us (87%)
  local copies, waits for them, and re-layouts  4.44 us (12%)
    pallas_call x1, Pallas kernels, on_device(): pl.pallas_call(functools.partial(kernel, n, slots), out_shape=jax.ShapeDt...  31 us
    unnamed x11, local copies, waits for them, and re-layouts  4.44 us

profile of v1, /device:TPU:0, one launch (start us, length us, event | category | flops | bytes accessed | tf_op | source)
XLA Modules:
  0.0 35.5 jit_solution(288825263279293830)
XLA Ops:
  0.0 0.0 copy-start
  0.0 1.1 %copy-done = f32[12,128,128]{2,1,0:T(8,128)S(1)} copy-done((f32[12,128,128]{2,1,0:T(8,128)S(1)}, f32[12,128,128]{2,1,0:T(8,128)}, u32[]{:S(2)}) %copy-start) | copy-done | bytes 786456
  1.1 0.0 copy-start.1
  1.1 0.7 %copy-done.1 = f32[12,128]{1,0:T(8,128)S(1)} copy-done((f32[12,128]{1,0:T(8,128)S(1)}, f32[12,128]{1,0:T(8,128)}, u32[]{:S(2)}) %copy-start.1) | copy-done | bytes 6168
  1.8 0.0 copy-start.2
  1.8 0.7 %copy-done.2 = f32[12,128]{1,0:T(8,128)S(1)} copy-done((f32[12,128]{1,0:T(8,128)S(1)}, f32[12,128]{1,0:T(8,128)}, u32[]{:S(2)}) %copy-start.2) | copy-done | bytes 6168
  2.5 0.0 copy-start.3
  2.5 0.7 %copy-done.3 = s32[96]{0:T(128)S(1)} copy-done((s32[96]{0:T(128)S(1)}, s32[96]{0:T(128)}, u32[]{:S(2)}) %copy-start.3) | copy-done | bytes 408
  3.2 0.0 copy-start.4
  3.2 0.7 %copy-done.4 = s32[96]{0:T(128)S(1)} copy-done((s32[96]{0:T(128)S(1)}, s32[96]{0:T(128)}, u32[]{:S(2)}) %copy-start.4) | copy-done | bytes 408
  3.8 31.0 %shard_map.64 = f32[12,128]{1,0:T(8,128)S(1)} custom-call(f32[12,128]{1,0:T(8,128)S(1)} %copy-done.1, f32[12,128]{1,0:T(8,128)S(1)} %copy-done.2, f32[12,128,128]{2,1,0:T(8,128)S(1)} %copy-done, f32[96,128,128]{2,1,0:T(8,128)} %coup_hbm.1, s32[1,96]{1,0:T(1,128)S(1)} %bitcast.2, s32[1,96]{1,0:T(1,128)S(1)} %bitcast.3), custom_call_target="tpu_custom_call" | custom-call | tf_op jit(solution)/shard_map/pallas_call | solution.py:437
  34.9 0.6 %copy.8 = f32[12,128]{1,0:T(8,128)} copy(f32[12,128]{1,0:T(8,128)S(1)} %shard_map.64) | data formatting | bytes 12288
Async XLA Ops:
  0.0 1.1 %copy-start = (f32[12,128,128]{2,1,0:T(8,128)S(1)}, f32[12,128,128]{2,1,0:T(8,128)}, u32[]{:S(2)}) copy-start(f32[12,128,128]{2,1,0:T(8,128)} %diag_hbm.1) | copy-start | bytes 2359300
  1.1 0.7 %copy-start.1 = (f32[12,128]{1,0:T(8,128)S(1)}, f32[12,128]{1,0:T(8,128)}, u32[]{:S(2)}) copy-start(f32[12,128]{1,0:T(8,128)} %defect_hbm.1) | copy-start | bytes 18436
  1.8 0.7 %copy-start.2 = (f32[12,128]{1,0:T(8,128)S(1)}, f32[12,128]{1,0:T(8,128)}, u32[]{:S(2)}) copy-start(f32[12,128]{1,0:T(8,128)} %mass_hbm.1) | copy-start | bytes 18436
  2.5 0.7 %copy-start.3 = (s32[96]{0:T(128)S(1)}, s32[96]{0:T(128)}, u32[]{:S(2)}) copy-start(s32[96]{0:T(128)} %param.10) | copy-start | bytes 1156
  3.2 0.7 %copy-start.4 = (s32[96]{0:T(128)S(1)}, s32[96]{0:T(128)}, u32[]{:S(2)}) copy-start(s32[96]{0:T(128)} %param.11) | copy-start | bytes 1156

commit v2 on v1

--- a/solution.py
+++ b/solution.py
@@ -12,7 +12,7 @@
 I32 = jnp.int32
 MESH = pl.DeviceIdType.MESH
 BASE = 64
-VMEM_LIMIT = 48 * 1024 * 1024
+VMEM_LIMIT = 57 * 1024 * 1024
 
 
 def iota(shape, axis):
@@ -65,6 +65,9 @@
     table_v,
     table,
     wbuf,
+    held,
+    far_t,
+    diag_t,
     codes,
     ask_ref,
     goal_ref,
@@ -80,6 +83,7 @@
     load_sems,
     table_sem,
     sent,
+    passed,
     got,
 ):
     me = lax.axis_index("blk")
@@ -203,8 +207,31 @@
         view = target.at[pl.ds(0, (n - 1) * size)]
         pltpu.make_async_copy(view, view, sent.at[phase]).wait()
 
+    core = me % 2
+
+    def first_copy(source, group, device, spot, size, sem):
+        return pltpu.make_async_remote_copy(
+            src_ref=source,
+            dst_ref=recv0.at[pl.ds(spot * head, size * head)],
+            send_sem=sem,
+            recv_sem=got.at[0, group],
+            device_id=(device,),
+            device_id_type=MESH,
+        )
+
     for group in range(count):
-        send(0, group, send0, recv0, head, False)
+        for place in range(groups[group][0], groups[group][1], 2):
+            if place < n - 2:
+                device, spot = peer[place + 1] + 1 - core, place + core
+            else:
+                device, spot = peer[place], place
+            first_copy(send0, group, device, spot, 1, sent.at[0]).start()
+
+    def pass_on(group):
+        first, last = groups[group]
+        last = min(last, n - 2)
+        part = recv0.at[pl.ds(first * head, (last - first) * head)]
+        return first_copy(part, group, peer[n - 2], first, last - first, passed)
 
     lane_k = iota((width, 128), 1)
     sub = iota((pad, 128), 0)
@@ -218,57 +245,35 @@
     def product(tile, row):
         return jnp.sum(tile * row, axis=1, keepdims=True)
 
-    def push_sums(group):
+    def spread(vector):
+        wbuf[...] = vector
+        filled = jnp.concatenate([vector, jnp.zeros((width - pad, 128), F32)], axis=0)
+        turned = filled.T
+        for index in range(rb):
+            held[index] = jnp.broadcast_to(turned[:, index : index + 1], (width, 128))
+
+    def push_group(turn, group):
+        for place, slot in slots_of(group):
+            line = place * slots + slot
+            value = far_t[line] * held[table[4, line]]
+            send_b[turn, line, :, :] = jnp.sum(value, axis=0, keepdims=True)
+        send(1 + 2 * turn, group, send_b.at[turn], recv_b.at[turn], slots, True)
+
+    def own_rows(image):
+        for index in range(rb):
+            value = jnp.sum(diag_t[index] * held[index], axis=0, keepdims=True)
+            image = image + jnp.where(sub == index, value, 0.0)
+        return image
+
+    def fetch_all(image, ready, source, between):
         acc = empty
-        for index, (place, slot) in enumerate(slots_of(group)):
-            line = place * slots + slot
-            row = wbuf[pl.ds(table[4, line], 1), :]
-            acc = jnp.where(lane_k == index, product(coup[table[3, line]], row), acc)
-        return acc
-
-    def push_out(turn, group, acc):
-        found = acc.T
-        for index, (place, slot) in enumerate(slots_of(group)):
-            send_b[turn, place * slots + slot, :, :] = found[index : index + 1, :]
-        send(1 + 2 * turn, group, send_b.at[turn], recv_b.at[turn], slots, True)
-
-    def push_all(turn):
-        held = push_sums(0)
-        for group in range(count):
-            later = push_sums(group + 1) if group + 1 < count else None
-            push_out(turn, group, held)
-            held = later
-
-    def fetch_sums(group, source):
-        acc = empty
-        for index, (place, slot) in enumerate(slots_of(group)):
-            line = place * slots + slot
-            row = source(place, slot)
-            acc = jnp.where(lane_k == index, product(coup[table[0, line]], row), acc)
-        return acc
-
-    def fetch_in(group, image, acc):
-        found = acc.T
-        for index, (place, slot) in enumerate(slots_of(group)):
-            here = sub == table[1, place * slots + slot]
-            image = image + jnp.where(here, found[index : index + 1, :], 0.0)
-        return image
-
-    def fetch_all(image, ready, source):
-        held = None
         for group in near_first:
             ready(group)
-            sums = fetch_sums(group, source)
-            if held is not None:
-                image = fetch_in(group + 1, image, held)
-            held = sums
-        return fetch_in(0, image, held)
-
-    def own_rows(image):
-        acc = empty
-        for index in range(rb):
-            value = product(diag[index], wbuf[index : index + 1, :])
-            acc = jnp.where(lane_k == index, value, acc)
+            for place, slot in slots_of(group):
+                line = place * slots + slot
+                value = product(coup[table[0, line]], source(place, slot))
+                acc = acc + jnp.where(lane_k == table[1, line], value, 0.0)
+            image = between(group, image)
         return image + acc.T[0:pad, :]
 
     def land_group(turn, group, image):
@@ -305,26 +310,50 @@
     table_copy.wait()
     mass = jnp.concatenate([mass_ref[...], jnp.zeros((pad - rb, 128), F32)], axis=0)
 
+    urgent = [group for group in range(count) if groups[group][0] < 8]
+    early = [group for group in reversed(range(count)) if groups[group][0] >= 8]
     near_first = list(reversed(range(count)))
-    push_all(0)
+    spread(vector)
+    for group in range(count):
+        for place, slot in slots_of(group):
+            line = place * slots + slot
+            far_t[line] = coup[table[3, line]].T
+        push_group(0, group)
+    for index in range(rb):
+        diag_t[index] = diag[index].T
     image = own_rows(mass * vector)
+    landed = {2: near_first[:2], 1: near_first[2:-2]} if count > 4 else {1: near_first[:-2]}
 
     def ready_first(group):
         await_group(0, group, recv0, head)
+        pl.when(core == 1)(pass_on(group).start)
         for place in range(*groups[group]):
-            codes[place : place + 1, :] = recv0[place * head + rb]
+            spot = place
+            if place < n - 2:
+                spot = place + (1 - core) * (1 - 2 * (place % 2))
+            codes[place : place + 1, :] = recv0[spot * head + rb]
             for row in range(rb):
-                blocks[place * rb + row, :, :] = recv0[place * head + row]
+                blocks[place * rb + row, :, :] = recv0[spot * head + row]
 
     def block_row(place, slot):
         return blocks[place * rb + table[2, place * slots + slot]]
 
-    image = fetch_all(image, ready_first, block_row)
-    decode(0, n)
+    def between_first(group, image):
+        if group == 1:
+            decode(8, n)
+            for other in early:
+                await_group(1, other, recv_b.at[0], slots)
+                image = land_group(0, other, image)
+        return image
+
+    image = fetch_all(image, ready_first, block_row, between_first)
+    decode(0, 8)
     whose = (n - 1 - iota((n, 128), 0)) ^ me
     squares = total(jnp.where(iota((n, 128), 1) == whose * slots, codes[...], 0.0))
     beta = jnp.sqrt(squares)
     for group in near_first:
+        if group in early:
+            continue
         await_group(1, group, recv_b.at[0], slots)
         image = land_group(0, group, image)
     basis = [vector / beta]
@@ -334,15 +363,21 @@
 
     for turn in range(1, ITERS):
         vector = images[-1]
-        wbuf[...] = vector
         own_part = as_row(
             [total(vector * item) for item in basis]
             + [total(vector * item) for item in images]
         )
-        for group in range(count):
+        for group in urgent:
             gather_group(turn, group, vector)
             send_asked(turn, group, own_part)
-        push_all(turn)
+        spread(vector)
+        for group in urgent:
+            push_group(turn, group)
+        for group in range(len(urgent), count):
+            gather_group(turn, group, vector)
+            send_asked(turn, group, own_part)
+        for group in range(len(urgent), count):
+            push_group(turn, group)
         image = own_rows(mass * vector)
         parts_of = [own_part]
 
@@ -354,7 +389,13 @@
         def asked_row(place, slot):
             return recv_a[turn - 1, place * lines + slot, :, :]
 
-        image = fetch_all(image, ready, asked_row)
+        def between(group, image):
+            for other in landed.get(group, ()):
+                await_group(1 + 2 * turn, other, recv_b.at[turn], slots)
+                image = land_group(turn, other, image)
+            return image
+
+        image = fetch_all(image, ready, asked_row, between)
         sums = sum(parts_of[1:], parts_of[0])
         dots = [pick(sums, index) for index in range(turn)]
         for index in range(turn):
@@ -368,7 +409,7 @@
         for index in range(turn):
             vector = vector - dots[index] * basis[index]
         basis.append(vector * scale)
-        for group in near_first:
+        for group in near_first[-2:]:
             await_group(1 + 2 * turn, group, recv_b.at[turn], slots)
             image = land_group(turn, group, image)
         for index in range(turn):
@@ -416,7 +457,10 @@
         update = update + mixing[i] * basis[i]
     out_ref[...] = update[0:rb, :]
 
-    await_sent(0, recv0, head)
+    view = recv0.at[pl.ds(0, n // 2 * head)]
+    pltpu.make_async_copy(view, view, sent.at[0]).wait()
+    whole = recv0.at[pl.ds(0, (n - 2) * head)]
+    pl.when(core == 1)(pltpu.make_async_copy(whole, whole, passed).wait)
     for turn in range(ITERS):
         await_sent(1 + 2 * turn, recv_b.at[turn], slots)
     for turn in range(1, ITERS):
@@ -436,7 +480,7 @@
     phases = 2 * ITERS + 1
     return pl.pallas_call(
         functools.partial(kernel, n, slots),
-        out_shape=jax.ShapeDtypeStruct((rb, width), F32),
+        out_shape=pltpu.VMEM((rb, width), F32),
         in_specs=[hbm] * 6,
         out_specs=pl.BlockSpec(memory_space=pltpu.VMEM),
         scratch_shapes=[
@@ -449,6 +493,9 @@
             pltpu.VMEM((8, lanes), I32),
             pltpu.SMEM((8, lanes), I32),
             pltpu.VMEM((pad, width), F32),
+            pltpu.VMEM((rb, width, width), F32),
+            pltpu.VMEM(((n - 1) * slots, width, width), F32),
+            pltpu.VMEM((rb, width, width), F32),
             pltpu.VMEM((n, width), F32),
             pltpu.VMEM((slots, n, width), F32),
             pltpu.VMEM((slots, n, width), F32),
@@ -464,6 +511,7 @@
             pltpu.SemaphoreType.DMA((9,)),
             pltpu.SemaphoreType.DMA,
             pltpu.SemaphoreType.DMA((phases,)),
+            pltpu.SemaphoreType.DMA,
             pltpu.SemaphoreType.DMA((phases, len(ranges(n)))),
         ],
         compiler_params=pltpu.CompilerParams(

time: 35.8 us -> 30.6 us (0.85)
  local copies, waits for them, and re-layouts: 4.44 us -> 0.6 us
  Pallas kernels: 31 us -> 29.8 us
    unnamed x11 -> x1, local copies, waits for them, and re-layouts: 4.44 us -> 0.6 us
    pallas_call x1, Pallas kernels: 31 us -> 29.8 us  [on_device(): pl.pallas_call(functools.partial(kernel, n, slots), out_shape=pltpu.VMEM(...]
where the time goes in v2:
time: 30.6 us; the launch traced here: 30.5 us
  Pallas kernels  29.8 us (97%)
  local copies, waits for them, and re-layouts  0.6 us (2%)
    pallas_call x1, Pallas kernels, on_device(): pl.pallas_call(functools.partial(kernel, n, slots), out_shape=pltpu.VMEM(...  29.8 us

profile of v2, /device:TPU:0, one launch (start us, length us, event | category | flops | bytes accessed | tf_op | source)
XLA Modules:
  0.0 30.5 jit_solution(9374856029636494318)
XLA Ops:
  0.0 29.8 %shard_map.64 = f32[12,128]{1,0:T(8,128)S(1)} custom-call(f32[12,128]{1,0:T(8,128)} %defect_hbm.1, f32[12,128]{1,0:T(8,128)} %mass_hbm.1, f32[12,128,128]{2,1,0:T(8,128)} %diag_hbm.1, f32[96,128,128]{2,1,0:T(8,128)} %coup_hbm.1, s32[1,96]{1,0:T(1,128)} %bitcast.2, s32[1,96]{1,0:T(1,128)} %bitcast.3), custom_call_target="tpu_custom_call" | custom-call | tf_op jit(solution)/shard_map/pallas_call | solution.py:481
  29.9 0.6 %copy.8 = f32[12,128]{1,0:T(8,128)} copy(f32[12,128]{1,0:T(8,128)S(1)} %shard_map.64) | data formatting | bytes 12288

commit v3 on v2

--- a/solution.py
+++ b/solution.py
@@ -40,10 +40,15 @@
     return jnp.sum(jnp.where(lane == index, row, 0.0), axis=1, keepdims=True)
 
 
-def ranges(n):
-    cuts = [0, 2, 6, 10, n // 2, n - n // 4, n - 1]
-    cuts = sorted({min(cut, n - 1) for cut in cuts})
-    return list(zip(cuts[:-1], cuts[1:]))
+def layout(n):
+    def far(chip):
+        return min((chip & 1) + (chip >> 1 & 1) + (chip >> 2), 5)
+
+    chips = sorted(range(n // 2), key=lambda chip: (-far(chip), -chip))
+    masks = [2 * chip + bit for chip in chips for bit in (1, 0)]
+    levels = [max(far(mask // 2), 1) for mask in masks[: n - 1]]
+    starts = [at for at in range(n - 1) if at == 0 or levels[at] != levels[at - 1]]
+    return masks, list(zip(starts, starts[1:] + [n - 1]))
 
 
 def kernel(
@@ -93,7 +98,7 @@
     lanes = table.shape[1]
     parts = 4
     chunk = tiles // parts
-    groups = ranges(n)
+    masks, groups = layout(n)
     count = len(groups)
     head = rb + 1
     lines = slots + 1
@@ -103,7 +108,7 @@
         low_bit = mask & -mask
         sign = 1 - 2 * ((me // low_bit) % 2)
         peers[mask] = peers[mask - low_bit] + sign * low_bit
-    peer = [peers[n - 1 - place] for place in range(n)]
+    peer = [peers[mask] for mask in masks]
 
     small = [
         pltpu.make_async_copy(rows_hbm, rows_ref, load_sems.at[parts + 1]),
@@ -149,7 +154,9 @@
     key_l = own_l + push_l * n
     key_s = to_s(key_l, 0)
     slot_l = jnp.sum(jnp.where((key_s == key_l) & earlier, 1, 0), axis=0, keepdims=True)
-    line_l = (n - 1 - (own_l ^ me)) * slots + slot_l
+    apart = own_l ^ me
+    place_l = sum(jnp.where(apart == mask, at, 0) for at, mask in enumerate(masks))
+    line_l = place_l * slots + slot_l
     tile_l = iota((1, tiles), 1)
     line_s = to_s(line_l + push_l * lanes, 0)
     pack_s = to_s(((tile_l * BASE + loc_l) * BASE + far_l) + 1, 0)
@@ -310,8 +317,9 @@
     table_copy.wait()
     mass = jnp.concatenate([mass_ref[...], jnp.zeros((pad - rb, 128), F32)], axis=0)
 
-    urgent = [group for group in range(count) if groups[group][0] < 8]
-    early = [group for group in reversed(range(count)) if groups[group][0] >= 8]
+    urgent = list(range(min(3, count)))
+    cut = min(-(-groups[min(1, count - 1)][1] // 8) * 8, n)
+    early = [group for group in reversed(range(count)) if groups[group][0] >= cut]
     near_first = list(reversed(range(count)))
     spread(vector)
     for group in range(count):
@@ -322,7 +330,7 @@
     for index in range(rb):
         diag_t[index] = diag[index].T
     image = own_rows(mass * vector)
-    landed = {2: near_first[:2], 1: near_first[2:-2]} if count > 4 else {1: near_first[:-2]}
+    landed = {2: near_first[:2], 1: near_first[2:-2]} if count > 3 else {1: near_first[:-2]}
 
     def ready_first(group):
         await_group(0, group, recv0, head)
@@ -340,15 +348,17 @@
 
     def between_first(group, image):
         if group == 1:
-            decode(8, n)
+            if cut < n:
+                decode(cut, n)
             for other in early:
                 await_group(1, other, recv_b.at[0], slots)
                 image = land_group(0, other, image)
         return image
 
     image = fetch_all(image, ready_first, block_row, between_first)
-    decode(0, 8)
-    whose = (n - 1 - iota((n, 128), 0)) ^ me
+    decode(0, cut)
+    places = iota((n, 1), 0)
+    whose = sum(jnp.where(places == at, mask, 0) for at, mask in enumerate(masks)) ^ me
     squares = total(jnp.where(iota((n, 128), 1) == whose * slots, codes[...], 0.0))
     beta = jnp.sqrt(squares)
     for group in near_first:
@@ -371,12 +381,12 @@
             gather_group(turn, group, vector)
             send_asked(turn, group, own_part)
         spread(vector)
-        for group in urgent:
+        for group in urgent[:2]:
             push_group(turn, group)
         for group in range(len(urgent), count):
             gather_group(turn, group, vector)
             send_asked(turn, group, own_part)
-        for group in range(len(urgent), count):
+        for group in range(len(urgent[:2]), count):
             push_group(turn, group)
         image = own_rows(mass * vector)
         parts_of = [own_part]
@@ -512,7 +522,7 @@
             pltpu.SemaphoreType.DMA,
             pltpu.SemaphoreType.DMA((phases,)),
             pltpu.SemaphoreType.DMA,
-            pltpu.SemaphoreType.DMA((phases, len(ranges(n)))),
+            pltpu.SemaphoreType.DMA((phases, len(layout(n)[1]))),
         ],
         compiler_params=pltpu.CompilerParams(
             collective_id=0, has_side_effects=True, vmem_limit_bytes=VMEM_LIMIT

time: 30.6 us -> 29.6 us (0.967)
  Pallas kernels: 29.8 us -> 28.8 us
    pallas_call x1, Pallas kernels: 29.8 us -> 28.8 us  [on_device(): pl.pallas_call(functools.partial(kernel, n, slots), out_shape=pltpu.VMEM(...]
where the time goes in v3:
time: 29.6 us; the launch traced here: 29.4 us
  Pallas kernels  28.8 us (97%)
  local copies, waits for them, and re-layouts  0.6 us (2%)
    pallas_call x1, Pallas kernels, on_device(): pl.pallas_call(functools.partial(kernel, n, slots), out_shape=pltpu.VMEM(...  28.8 us
    unnamed x1, local copies, waits for them, and re-layouts  0.6 us

profile of v3, /device:TPU:0, one launch (start us, length us, event | category | flops | bytes accessed | tf_op | source)
XLA Modules:
  0.0 29.4 jit_solution(4975117587198717650)
XLA Ops:
  0.0 28.8 %shard_map.64 = f32[12,128]{1,0:T(8,128)S(1)} custom-call(f32[12,128]{1,0:T(8,128)} %defect_hbm.1, f32[12,128]{1,0:T(8,128)} %mass_hbm.1, f32[12,128,128]{2,1,0:T(8,128)} %diag_hbm.1, f32[96,128,128]{2,1,0:T(8,128)} %coup_hbm.1, s32[1,96]{1,0:T(1,128)} %bitcast.2, s32[1,96]{1,0:T(1,128)} %bitcast.3), custom_call_target="tpu_custom_call" | custom-call | tf_op jit(solution)/shard_map/pallas_call | solution.py:491
  28.8 0.6 %copy.8 = f32[12,128]{1,0:T(8,128)} copy(f32[12,128]{1,0:T(8,128)S(1)} %shard_map.64) | data formatting | bytes 12288

commit v4 on v3

--- a/solution.py
+++ b/solution.py
@@ -252,10 +252,11 @@
     def product(tile, row):
         return jnp.sum(tile * row, axis=1, keepdims=True)
 
-    def spread(vector):
-        wbuf[...] = vector
+    def turn_over(vector):
         filled = jnp.concatenate([vector, jnp.zeros((width - pad, 128), F32)], axis=0)
-        turned = filled.T
+        return filled.T
+
+    def spread(turned):
         for index in range(rb):
             held[index] = jnp.broadcast_to(turned[:, index : index + 1], (width, 128))
 
@@ -266,6 +267,16 @@
             send_b[turn, line, :, :] = jnp.sum(value, axis=0, keepdims=True)
         send(1 + 2 * turn, group, send_b.at[turn], recv_b.at[turn], slots, True)
 
+    ones = jnp.ones((2 * width, 128), jnp.bfloat16)
+
+    def product_too(tile, row):
+        value = tile * row
+        high = value.astype(jnp.bfloat16)
+        rest = (value - high.astype(F32)).astype(jnp.bfloat16)
+        return jnp.dot(
+            jnp.concatenate([high, rest], axis=1), ones, preferred_element_type=F32
+        )
+
     def own_rows(image):
         for index in range(rb):
             value = jnp.sum(diag_t[index] * held[index], axis=0, keepdims=True)
@@ -276,9 +287,10 @@
         acc = empty
         for group in near_first:
             ready(group)
-            for place, slot in slots_of(group):
+            for index, (place, slot) in enumerate(slots_of(group)):
                 line = place * slots + slot
-                value = product(coup[table[0, line]], source(place, slot))
+                by = product_too if group > 0 and index % 3 == 1 else product
+                value = by(coup[table[0, line]], source(place, slot))
                 acc = acc + jnp.where(lane_k == table[1, line], value, 0.0)
             image = between(group, image)
         return image + acc.T[0:pad, :]
@@ -317,11 +329,11 @@
     table_copy.wait()
     mass = jnp.concatenate([mass_ref[...], jnp.zeros((pad - rb, 128), F32)], axis=0)
 
-    urgent = list(range(min(3, count)))
+    urgent = list(range(count))
     cut = min(-(-groups[min(1, count - 1)][1] // 8) * 8, n)
     early = [group for group in reversed(range(count)) if groups[group][0] >= cut]
     near_first = list(reversed(range(count)))
-    spread(vector)
+    spread(turn_over(vector))
     for group in range(count):
         for place, slot in slots_of(group):
             line = place * slots + slot
@@ -377,10 +389,11 @@
             [total(vector * item) for item in basis]
             + [total(vector * item) for item in images]
         )
+        turned = turn_over(vector)
         for group in urgent:
             gather_group(turn, group, vector)
             send_asked(turn, group, own_part)
-        spread(vector)
+        spread(turned)
         for group in urgent[:2]:
             push_group(turn, group)
         for group in range(len(urgent), count):
@@ -434,6 +447,30 @@
     last_phase = 2 * ITERS
     for group in range(count):
         send(last_phase, group, send_f, recv_f, 1, False)
+    view = recv0.at[pl.ds(0, n // 2 * head)]
+    pltpu.make_async_copy(view, view, sent.at[0]).wait()
+    whole = recv0.at[pl.ds(0, (n - 2) * head)]
+    pl.when(core == 1)(pltpu.make_async_copy(whole, whole, passed).wait)
+    for turn in range(ITERS):
+        await_sent(1 + 2 * turn, recv_b.at[turn], slots)
+    for turn in range(1, ITERS):
+        await_sent(2 * turn, recv_a.at[turn - 1], lines)
+    factor = {}
+    forward = []
+
+    def eliminate(i):
+        for j in range(i + 1):
+            value = gram[j, i]
+            for k in range(j):
+                value = value - factor[i, k] * factor[j, k]
+            factor[i, j] = jnp.sqrt(value) if i == j else value / factor[j, j]
+        value = beta * heads[i]
+        for k in range(i):
+            value = value - factor[i, k] * forward[k]
+        forward.append(value / factor[i, i])
+
+    for i in range(ITERS - 1):
+        eliminate(i)
     sums = own_part
     for group in near_first:
         await_group(last_phase, group, recv_f, 1)
@@ -443,19 +480,7 @@
     for index in range(ITERS):
         gram[index, ITERS - 1] = pick(sums, 1 + index)
 
-    factor = {}
-    for i in range(ITERS):
-        for j in range(i + 1):
-            value = gram[j, i]
-            for k in range(j):
-                value = value - factor[i, k] * factor[j, k]
-            factor[i, j] = jnp.sqrt(value) if i == j else value / factor[j, j]
-    forward = []
-    for i in range(ITERS):
-        value = beta * heads[i]
-        for k in range(i):
-            value = value - factor[i, k] * forward[k]
-        forward.append(value / factor[i, i])
+    eliminate(ITERS - 1)
     mixing = [None] * ITERS
     for i in reversed(range(ITERS)):
         value = forward[i]
@@ -467,14 +492,6 @@
         update = update + mixing[i] * basis[i]
     out_ref[...] = update[0:rb, :]
 
-    view = recv0.at[pl.ds(0, n // 2 * head)]
-    pltpu.make_async_copy(view, view, sent.at[0]).wait()
-    whole = recv0.at[pl.ds(0, (n - 2) * head)]
-    pl.when(core == 1)(pltpu.make_async_copy(whole, whole, passed).wait)
-    for turn in range(ITERS):
-        await_sent(1 + 2 * turn, recv_b.at[turn], slots)
-    for turn in range(1, ITERS):
-        await_sent(2 * turn, recv_a.at[turn - 1], lines)
     await_sent(last_phase, recv_f, 1)
 
 

time: 29.6 us -> 29.2 us (0.986)
  Pallas kernels: 28.8 us -> 28.5 us
    pallas_call x1, Pallas kernels: 28.8 us -> 28.5 us  [on_device(): pl.pallas_call(functools.partial(kernel, n, slots), out_shape=pltpu.VMEM(...]
where the time goes in v4:
time: 29.2 us; the launch traced here: 29.1 us
  Pallas kernels  28.5 us (98%)
  local copies, waits for them, and re-layouts  0.6 us (2%)
    pallas_call x1, Pallas kernels, on_device(): pl.pallas_call(functools.partial(kernel, n, slots), out_shape=pltpu.VMEM(...  28.5 us
    unnamed x1, local copies, waits for them, and re-layouts  0.6 us

profile of v4, /device:TPU:0, one launch (start us, length us, event | category | flops | bytes accessed | tf_op | source)
XLA Modules:
  0.0 29.1 jit_solution(1109457086861099069)
XLA Ops:
  0.0 28.5 %shard_map.64 = f32[12,128]{1,0:T(8,128)S(1)} custom-call(f32[12,128]{1,0:T(8,128)} %defect_hbm.1, f32[12,128]{1,0:T(8,128)} %mass_hbm.1, f32[12,128,128]{2,1,0:T(8,128)} %diag_hbm.1, f32[96,128,128]{2,1,0:T(8,128)} %coup_hbm.1, s32[1,96]{1,0:T(1,128)} %bitcast.2, s32[1,96]{1,0:T(1,128)} %bitcast.3), custom_call_target="tpu_custom_call" | custom-call | tf_op jit(solution)/shard_map/pallas_call | solution.py:508
  28.5 0.6 %copy.8 = f32[12,128]{1,0:T(8,128)} copy(f32[12,128]{1,0:T(8,128)S(1)} %shard_map.64) | data formatting | bytes 12288

commit v5 on v4

--- a/solution.py
+++ b/solution.py
@@ -226,7 +226,12 @@
             device_id_type=MESH,
         )
 
+    plain = [count - 1]
     for group in range(count):
+        if group in plain:
+            for place in range(*groups[group]):
+                first_copy(send0, group, peer[place], place, 1, sent.at[0]).start()
+            continue
         for place in range(groups[group][0], groups[group][1], 2):
             if place < n - 2:
                 device, spot = peer[place + 1] + 1 - core, place + core
@@ -345,11 +350,19 @@
     landed = {2: near_first[:2], 1: near_first[2:-2]} if count > 3 else {1: near_first[:-2]}
 
     def ready_first(group):
+        if group == 1:
+            take_first(1)
+            take_first(0)
+        elif group > 1 or count == 1:
+            take_first(group)
+
+    def take_first(group):
         await_group(0, group, recv0, head)
-        pl.when(core == 1)(pass_on(group).start)
+        if group not in plain:
+            pl.when(core == 1)(pass_on(group).start)
         for place in range(*groups[group]):
             spot = place
-            if place < n - 2:
+            if place < n - 2 and group not in plain:
                 spot = place + (1 - core) * (1 - 2 * (place % 2))
             codes[place : place + 1, :] = recv0[spot * head + rb]
             for row in range(rb):
@@ -359,7 +372,7 @@
         return blocks[place * rb + table[2, place * slots + slot]]
 
     def between_first(group, image):
-        if group == 1:
+        if group == 0:
             if cut < n:
                 decode(cut, n)
             for other in early:
@@ -447,9 +460,10 @@
     last_phase = 2 * ITERS
     for group in range(count):
         send(last_phase, group, send_f, recv_f, 1, False)
-    view = recv0.at[pl.ds(0, n // 2 * head)]
+    extra = n - 2 - groups[plain[0]][0]
+    view = recv0.at[pl.ds(0, (n // 2 + extra // 2) * head)]
     pltpu.make_async_copy(view, view, sent.at[0]).wait()
-    whole = recv0.at[pl.ds(0, (n - 2) * head)]
+    whole = recv0.at[pl.ds(0, (n - 2 - extra) * head)]
     pl.when(core == 1)(pltpu.make_async_copy(whole, whole, passed).wait)
     for turn in range(ITERS):
         await_sent(1 + 2 * turn, recv_b.at[turn], slots)

time: 29.2 us -> 29.1 us (level)
  no operation moved by 1% of the time
where the time goes in v5:
time: 29.1 us; the launch traced here: 29 us
  Pallas kernels  28.4 us (98%)
  local copies, waits for them, and re-layouts  0.6 us (2%)
    pallas_call x1, Pallas kernels, on_device(): pl.pallas_call(functools.partial(kernel, n, slots), out_shape=pltpu.VMEM(...  28.4 us
    unnamed x1, local copies, waits for them, and re-layouts  0.6 us

profile of v5, /device:TPU:0, one launch (start us, length us, event | category | flops | bytes accessed | tf_op | source)
XLA Modules:
  0.0 29.0 jit_solution(2413840173769906982)
XLA Ops:
  0.0 28.4 %shard_map.64 = f32[12,128]{1,0:T(8,128)S(1)} custom-call(f32[12,128]{1,0:T(8,128)} %defect_hbm.1, f32[12,128]{1,0:T(8,128)} %mass_hbm.1, f32[12,128,128]{2,1,0:T(8,128)} %diag_hbm.1, f32[96,128,128]{2,1,0:T(8,128)} %coup_hbm.1, s32[1,96]{1,0:T(1,128)} %bitcast.2, s32[1,96]{1,0:T(1,128)} %bitcast.3), custom_call_target="tpu_custom_call" | custom-call | tf_op jit(solution)/shard_map/pallas_call | solution.py:522
  28.4 0.6 %copy.8 = f32[12,128]{1,0:T(8,128)} copy(f32[12,128]{1,0:T(8,128)S(1)} %shard_map.64) | data formatting | bytes 12288

commit v6 on v5

--- a/solution.py
+++ b/solution.py
@@ -226,7 +226,7 @@
             device_id_type=MESH,
         )
 
-    plain = [count - 1]
+    plain = [group for group in range(count) if group >= count - 2]
     for group in range(count):
         if group in plain:
             for place in range(*groups[group]):

time: 29.1 us -> 29.1 us (level)
  no operation moved by 1% of the time
where the time goes in v6:
time: 29.1 us; the launch traced here: 29 us
  Pallas kernels  28.3 us (97%)
  local copies, waits for them, and re-layouts  0.6 us (2%)
    pallas_call x1, Pallas kernels, on_device(): pl.pallas_call(functools.partial(kernel, n, slots), out_shape=pltpu.VMEM(...  28.3 us
    unnamed x1, local copies, waits for them, and re-layouts  0.6 us

profile of v6, /device:TPU:0, one launch (start us, length us, event | category | flops | bytes accessed | tf_op | source)
XLA Modules:
  0.0 29.0 jit_solution(7582370343598754922)
XLA Ops:
  0.0 28.3 %shard_map.64 = f32[12,128]{1,0:T(8,128)S(1)} custom-call(f32[12,128]{1,0:T(8,128)} %defect_hbm.1, f32[12,128]{1,0:T(8,128)} %mass_hbm.1, f32[12,128,128]{2,1,0:T(8,128)} %diag_hbm.1, f32[96,128,128]{2,1,0:T(8,128)} %coup_hbm.1, s32[1,96]{1,0:T(1,128)} %bitcast.2, s32[1,96]{1,0:T(1,128)} %bitcast.3), custom_call_target="tpu_custom_call" | custom-call | tf_op jit(solution)/shard_map/pallas_call | solution.py:522
  28.4 0.6 %copy.8 = f32[12,128]{1,0:T(8,128)} copy(f32[12,128]{1,0:T(8,128)S(1)} %shard_map.64) | data formatting | bytes 12288
